TPU v7x, 256 devices: a whole 4x4x8 slice. The times are simulated.
256 devices in a mesh: inst: 4 (over x_hi, core), gx: 8 (over y, x_lo), gy: 8 (over z).
Axes of the slice: x: 4 (x_hi: 2, x_lo: 2; x = x_hi * 2 + x_lo), y: 4, z: 8, core: 2. Of those that a mesh axis runs over, the one named last changes fastest.
Arguments:
- state: float32 [8, 5, 64, 64, 128], P('inst', None, 'gx', 'gy'), may hold values from -6 to 6
- source: float32 [8, 5, 64, 64, 128], P('inst', None, 'gx', 'gy'), may hold values from -60 to 60
- jacobian: float32 [8, 5, 5, 64, 64, 128], P('inst', None, None, 'gx', 'gy'), may hold values from -1.5 to 16, as said below
- couplings: float32 [6, 5, 5], replicated, may hold values from -0.625 to 0.625
- omega: float32 [1], replicated, may hold values from 0.2 to 0.6
Outputs:
- state_next: float32 [8, 5, 64, 64, 128], P('inst', None, 'gx', 'gy')
- last_residual: float32 [8, 5, 64, 64, 128], P('inst', None, 'gx', 'gy')
Inputs may be any that keep to these rules, and one draw needn't show every extreme that they name: In every block jacobian[n, :, :, cell] each diagonal entry lies in 8 to 16 and exceeds the sum of magnitudes of the other entries of its row by 2 or more.
All inputs are finite; a program needn't handle non-finite values.
Results may differ from a plain program's by a relative error of at most 0.0003.
Values sent between devices are 32-bit elements; how exact they have to be, the bound alone decides.
A program may use at most 64 MiB of HBM per device.

v0:
```python
import functools
import math

import jax
import jax.numpy as jnp
from jax import lax
from jax.experimental import pallas as pl
from jax.experimental.pallas import tpu as pltpu
from jax.sharding import PartitionSpec as P

ITERS = 3
NV = 5
MESH = pl.DeviceIdType.MESH


def table_value(offset, total):
    angle = math.pi * offset / total
    return 0.5 * (-1.0) ** offset * math.cos(angle) / math.sin(angle)


def kernel(
    state_ref, source_ref, jac_ref, coup_ref, omega_ref,
    out_ref, res_ref,
    cur, src, jac, lu, near, far, fwd, ysend, yrecv, resid, cs,
    load_sem, src_sem, jac_sem, near_sem, far_sem, fwd_sem, y_sem, gx_sem, send_sem, out_sem,
):
    inst, gx, gy = lax.axis_index("inst"), lax.axis_index("gx"), lax.axis_index("gy")
    ngx, ngy, ranks = lax.axis_size("gx"), lax.axis_size("gy"), lax.axis_size("inst")
    nloc, nx = state_ref.shape[0], state_ref.shape[2]
    total = ranks * nloc
    parity = lax.rem(inst, 2)
    other_core = (inst + 1 - 2 * parity, gx, gy)
    other_chip = (lax.rem(inst + 2, ranks), gx, gy)
    gx_low, gx_high = (inst, gx - 1, gy), (inst, gx + 1, gy)
    gy_low = (inst, gx, lax.rem(gy + ngy - 1, ngy))
    gy_high = (inst, gx, lax.rem(gy + 1, ngy))
    has_low, has_high = gx > 0, gx < ngx - 1

    def plane_at(position):
        half = position // 2
        odd = position - 2 * half
        return half + odd * (nx - 1 - 2 * half)

    def load_state(x):
        return pltpu.make_async_copy(state_ref.at[:, :, x], cur.at[0, x + 1], load_sem.at[x])

    def remote(source, target, send, recv, device):
        return pltpu.make_async_remote_copy(
            src_ref=source, dst_ref=target, send_sem=send, recv_sem=recv,
            device_id=device, device_id_type=MESH,
        )

    def near_copy(k, x):
        return remote(cur.at[k, x + 1], near.at[k, x], send_sem.at[0], near_sem.at[k, x], other_core)

    def far_copy(k, x):
        return remote(cur.at[k, x + 1], far.at[k, x], send_sem.at[1], far_sem.at[k, x], other_chip)

    def fwd_copy(k, x):
        return remote(far.at[k, x], fwd.at[k, x], send_sem.at[2], fwd_sem.at[k, x], other_core)

    def y_copy(k, x, d):
        return remote(
            ysend.at[k, x, d], yrecv.at[k, x, d], send_sem.at[3 + d], y_sem.at[k, x, d],
            gy_high if d == 0 else gy_low,
        )

    def gx_copy(k, d):
        if d == 0:
            return remote(cur.at[k, nx], cur.at[k, 0], send_sem.at[5], gx_sem.at[k, 0], gx_high)
        return remote(cur.at[k, 1], cur.at[k, nx + 1], send_sem.at[6], gx_sem.at[k, 1], gx_low)

    def send_plane(k, x):
        far_copy(k, x).start()

        @pl.when((x == 0) & has_low)
        def _():
            gx_copy(k, 1).start()

        @pl.when((x == nx - 1) & has_high)
        def _():
            gx_copy(k, 0).start()

        near_copy(k, x).start()
        y_copy(k, x, 0).start()
        y_copy(k, x, 1).start()

    def start_load(p, c):
        load_state(plane_at(p)).start()
        return c

    lax.fori_loop(0, nx, start_load, 0)
    for n in range(nloc):
        pltpu.make_async_copy(jac_ref.at[n], jac.at[n], jac_sem.at[n]).start()
    pltpu.make_async_copy(source_ref, src, src_sem).start()

    barrier = pltpu.get_barrier_semaphore()
    for device in (other_core, other_chip, gy_low, gy_high):
        pl.semaphore_signal(barrier, inc=1, device_id=device, device_id_type=MESH)

    @pl.when(has_low)
    def _():
        pl.semaphore_signal(barrier, inc=1, device_id=gx_low, device_id_type=MESH)

    @pl.when(has_high)
    def _():
        pl.semaphore_signal(barrier, inc=1, device_id=gx_high, device_id_type=MESH)

    tile = cs.shape[1:]
    for d in range(6):
        for v in range(NV):
            for w in range(NV):
                cs[(d * NV + v) * NV + w] = jnp.full(tile, coup_ref[d, v, w], jnp.float32)
    zeros = jnp.zeros(cur.shape[2:], jnp.float32)

    @pl.when(gx == 0)
    def _():
        for k in range(ITERS):
            cur[k, 0] = zeros

    @pl.when(gx == ngx - 1)
    def _():
        for k in range(ITERS):
            cur[k, nx + 1] = zeros

    pl.semaphore_wait(barrier, 4 + has_low.astype(jnp.int32) + has_high.astype(jnp.int32))

    def put_rows(k, x, n, v, plane):
        ysend[k, x, 0, n, v : v + 1, :] = plane[7:8, :]
        ysend[k, x, 1, n, v : v + 1, :] = plane[0:1, :]

    def first_send(p, c):
        x = plane_at(p)
        load_state(x).wait()
        for n in range(nloc):
            for v in range(NV):
                put_rows(0, x, n, v, cur[0, x + 1, n, v])
        send_plane(0, x)
        return c

    lax.fori_loop(0, nx, first_send, 0)

    for n in range(nloc):
        pltpu.make_async_copy(jac_ref.at[n], jac.at[n], jac_sem.at[n]).wait()

    def factor(x, c):
        for n in range(nloc):
            m = [[jac[n, i, j, x] for j in range(NV)] for i in range(NV)]
            for p in range(NV):
                m[p][p] = 1.0 / m[p][p]
                for t in range(p + 1, NV):
                    m[t][p] = m[t][p] * m[p][p]
                    for j in range(p + 1, NV):
                        m[t][j] = m[t][j] - m[t][p] * m[p][j]
            for i in range(NV):
                for j in range(NV):
                    lu[n, i, j, x] = m[i][j]
        return c

    lax.fori_loop(0, nx, factor, 0)
    pltpu.make_async_copy(source_ref, src, src_sem).wait()

    omega = omega_ref[0]

    def weight(even, odd):
        return omega * jnp.where(parity == 0, jnp.float32(even), jnp.float32(odd))

    value = functools.partial(table_value, total=total)
    own_w = [[None if j == m else omega * jnp.float32(value(j - m)) for m in range(nloc)] for j in range(nloc)]
    near_w = [[weight(value(j - m - 2), value(j - m + 2)) for m in range(nloc)] for j in range(nloc)]
    far_w = [[omega * jnp.float32(value(j - m + 4)) for m in range(nloc)] for j in range(nloc)]
    fwd_w = [[weight(value(j - m + 2), value(j - m - 2)) for m in range(nloc)] for j in range(nloc)]

    def forward(step):
        k = step // nx
        x = plane_at(step - k * nx)
        far_copy(k, x).wait_recv()
        fwd_copy(k, x).start()

    def output_copies(x):
        return (
            pltpu.make_async_copy(cur.at[ITERS, x + 1], out_ref.at[:, :, x], out_sem.at[0, x]),
            pltpu.make_async_copy(resid.at[x], res_ref.at[:, :, x], out_sem.at[1, x]),
        )

    def compute(step):
        k = step // nx
        x = plane_at(step - k * nx)
        near_copy(k, x).wait_recv()
        y_copy(k, x, 0).wait_recv()
        y_copy(k, x, 1).wait_recv()

        @pl.when((x == 0) & has_low)
        def _():
            gx_copy(k, 0).wait_recv()

        @pl.when((x == nx - 1) & has_high)
        def _():
            gx_copy(k, 1).wait_recv()

        fwd_copy(k, x).wait_recv()

        lane = lax.broadcasted_iota(jnp.int32, tile, 1)
        row = lax.broadcasted_iota(jnp.int32, tile, 0)
        ny, nz = tile
        pairs = [(n, v) for n in range(nloc) for v in range(NV)]

        def shifted(d, n, w):
            if d < 2:
                return cur[k, x + 2 * d, n, w]
            plane = cur[k, x + 1, n, w]
            if d == 2:
                return jnp.where(row == 0, yrecv[k, x, 0, n, w : w + 1, :], pltpu.roll(plane, 1, 0))
            if d == 3:
                return jnp.where(row == ny - 1, yrecv[k, x, 1, n, w : w + 1, :], pltpu.roll(plane, ny - 1, 0))
            if d == 4:
                return jnp.where(lane == 0, 0.0, pltpu.roll(plane, 1, 1))
            return jnp.where(lane == nz - 1, 0.0, pltpu.roll(plane, nz - 1, 1))

        total_of = {}
        for n, v in pairs:
            total_of[n, v] = src[n, v, x]
        for n in range(nloc):
            mine = [cur[k, x + 1, n, w] for w in range(NV)]
            for v in range(NV):
                for w in range(NV):
                    total_of[n, v] = total_of[n, v] - jac[n, v, w, x] * mine[w]
        for d in range(6):
            field = {(n, w): shifted(d, n, w) for n, w in pairs}
            for v in range(NV):
                for w in range(NV):
                    c = cs[(d * NV + v) * NV + w]
                    for n in range(nloc):
                        total_of[n, v] = total_of[n, v] - c * field[n, w]
        for v in range(NV):
            own = [cur[k, x + 1, m, v] for m in range(nloc)]
            beside = [near[k, x, m, v] for m in range(nloc)]
            across = [far[k, x, m, v] for m in range(nloc)]
            relayed = [fwd[k, x, m, v] for m in range(nloc)]
            for j in range(nloc):
                acc = total_of[j, v]
                for weights, values in ((own_w, own), (near_w, beside), (far_w, across), (fwd_w, relayed)):
                    for m in range(nloc):
                        if weights[j][m] is not None:
                            acc = acc - weights[j][m] * values[m]
                total_of[j, v] = acc
        for n in range(nloc):
            b = [total_of[n, v] for v in range(NV)]
            for v in range(NV):
                resid[x, n, v] = b[v]
            for p in range(NV):
                for t in range(p + 1, NV):
                    b[t] = b[t] - lu[n, t, p, x] * b[p]
            for p in reversed(range(NV)):
                for j in range(p + 1, NV):
                    b[p] = b[p] - lu[n, p, j, x] * b[j]
                b[p] = b[p] * lu[n, p, p, x]
            for v in range(NV):
                plane = cur[k, x + 1, n, v] + b[v]
                cur[k + 1, x + 1, n, v] = plane
                put_rows(k + 1, x, n, v, plane)

        @pl.when(k < ITERS - 1)
        def _():
            send_plane(k + 1, x)

        @pl.when(k == ITERS - 1)
        def _():
            for copy in output_copies(x):
                copy.start()

    forward(0)

    def one_step(step, c):
        @pl.when(step + 1 < ITERS * nx)
        def _():
            forward(step + 1)

        compute(step)
        return c

    lax.fori_loop(0, ITERS * nx, one_step, 0)

    remote(near, near, send_sem.at[0], near_sem.at[0, 0], other_core).wait_send()
    remote(far, far, send_sem.at[1], far_sem.at[0, 0], other_chip).wait_send()
    remote(fwd, fwd, send_sem.at[2], fwd_sem.at[0, 0], other_core).wait_send()
    for d in range(2):
        sent = yrecv.at[:, :, d]
        remote(sent, sent, send_sem.at[3 + d], y_sem.at[0, 0, d], gy_high).wait_send()

    planes = near.at[0, pl.ds(0, ITERS)]

    @pl.when(has_high)
    def _():
        remote(planes, planes, send_sem.at[5], gx_sem.at[0, 0], gx_high).wait_send()

    @pl.when(has_low)
    def _():
        remote(planes, planes, send_sem.at[6], gx_sem.at[0, 1], gx_low).wait_send()

    def finish(x, c):
        for copy in output_copies(x):
            copy.wait()
        return c

    lax.fori_loop(0, nx, finish, 0)


def shards(state, source, jacobian, couplings, omega):
    nloc, nv, nx, ny, nz = state.shape
    whole = pl.BlockSpec(memory_space=pl.ANY)
    scalars = pl.BlockSpec(memory_space=pltpu.SMEM)
    f32 = jnp.float32
    dma = pltpu.SemaphoreType.DMA
    plane = (nloc, nv, ny, nz)
    out = jax.ShapeDtypeStruct(state.shape, f32)
    return pl.pallas_call(
        kernel,
        out_shape=(out, out),
        in_specs=[whole, whole, whole, scalars, scalars],
        out_specs=(whole, whole),
        scratch_shapes=[
            pltpu.VMEM((ITERS + 1, nx + 2) + plane, f32),
            pltpu.VMEM(source.shape, f32),
            pltpu.VMEM(jacobian.shape, f32),
            pltpu.VMEM(jacobian.shape, f32),
            pltpu.VMEM((ITERS, nx) + plane, f32),
            pltpu.VMEM((ITERS, nx) + plane, f32),
            pltpu.VMEM((ITERS, nx) + plane, f32),
            pltpu.VMEM((ITERS + 1, nx, 2, nloc, 8, nz), f32),
            pltpu.VMEM((ITERS, nx, 2, nloc, 8, nz), f32),
            pltpu.VMEM((nx,) + plane, f32),
            pltpu.VMEM((6 * NV * NV, ny, nz), f32),
            dma((nx,)),
            dma,
            dma((nloc,)),
            dma((ITERS, nx)),
            dma((ITERS, nx)),
            dma((ITERS, nx)),
            dma((ITERS, nx, 2)),
            dma((ITERS, 2)),
            dma((7,)),
            dma((2, nx)),
        ],
        compiler_params=pltpu.CompilerParams(collective_id=0, has_side_effects=True),
    )(state, source, jacobian, couplings, omega)


def solution(mesh):
    return jax.shard_map(
        shards,
        mesh=mesh,
        in_specs=(
            P("inst", None, "gx", "gy", None),
            P("inst", None, "gx", "gy", None),
            P("inst", None, None, "gx", "gy", None),
            P(),
            P(),
        ),
        out_specs=(P("inst", None, "gx", "gy", None), P("inst", None, "gx", "gy", None)),
        check_vma=False,
    )
```

profile of v0, /device:TPU:9, one launch (start us, length us, event | category | flops | bytes accessed | tf_op | source)
XLA Modules:
  0.0 46.6 jit_solution(10964449435810399204)
XLA Ops:
  1.3 1.3 %copy.7.coup_ref = f32[6,5,5]{2,1,0:T(8,128)} copy(f32[6,5,5]{2,0,1:T(8,128)} %param.8) | data formatting | bytes 1200 | tf_op args[3]
  2.6 40.5 %shard_map.68 = (f32[2,5,8,8,128]{4,3,2,1,0:T(8,128)}, f32[2,5,8,8,128]{4,3,2,1,0:T(8,128)}) custom-call(f32[2,5,8,8,128]{4,3,2,1,0:T(8,128)} %state_ref.1, f32[2,5,8,8,128]{4,3,2,1,0:T(8,128)} %source_ref.1, f32[2,5,5,8,8,128]{5,4,3,2,1,0:T(8,128)} %jac_ref.1, f32[6,5,5]{2,1,0:T(8,128)} %copy.7.coup_ref, f32[1]{0:T(128)S(6)} %copy.10.omega_ref), custom_call_target="tpu_custom_call" | custom-call | tf_op jit(solution)/shard_map/pallas_call | solution.py:317
  43.2 1.7 %copy.11 = f32[2,5,8,8,128]{4,3,2,1,0:T(8,128)} copy(f32[2,5,8,8,128]{4,3,2,1,0:T(8,128)} %get-tuple-element.4) | data formatting | bytes 655360
  44.9 1.7 %copy.12 = f32[2,5,8,8,128]{4,3,2,1,0:T(8,128)} copy(f32[2,5,8,8,128]{4,3,2,1,0:T(8,128)} %get-tuple-element.5) | data formatting | bytes 655360
where the time goes:
time: 46.9 us; the launch traced here: 46.6 us
  Pallas kernels  40.5 us (86%)
  local copies, waits for them, and re-layouts  4.78 us (10%)
  between operations  1.29 us (3%)
    pallas_call x1, Pallas kernels, shards(): pl.pallas_call(kernel, out_shape=(out, out), in_specs=[whole, whole, whol...  40.5 us
    unnamed x3, local copies, waits for them, and re-layouts  4.78 us

commit v1 on v0

--- a/solution.py
+++ b/solution.py
@@ -9,6 +9,7 @@
 from jax.sharding import PartitionSpec as P
 
 ITERS = 3
+OUTER_FIRST, OUTER_STEP, RELAY_LAG = 3, 2, 4
 NV = 5
 MESH = pl.DeviceIdType.MESH
 
@@ -21,8 +22,8 @@
 def kernel(
     state_ref, source_ref, jac_ref, coup_ref, omega_ref,
     out_ref, res_ref,
-    cur, src, jac, lu, near, far, fwd, ysend, yrecv, resid, cs,
-    load_sem, src_sem, jac_sem, near_sem, far_sem, fwd_sem, y_sem, gx_sem, send_sem, out_sem,
+    cur, src, jac, lu, near, far, fwd, ysend, yrecv, cs,
+    load_sem, src_sem, jac_sem, near_sem, far_sem, fwd_sem, y_sem, gx_sem, send_sem,
 ):
     inst, gx, gy = lax.axis_index("inst"), lax.axis_index("gx"), lax.axis_index("gy")
     ngx, ngy, ranks = lax.axis_size("gx"), lax.axis_size("gy"), lax.axis_size("inst")
@@ -31,15 +32,22 @@
     parity = lax.rem(inst, 2)
     other_core = (inst + 1 - 2 * parity, gx, gy)
     other_chip = (lax.rem(inst + 2, ranks), gx, gy)
-    gx_low, gx_high = (inst, gx - 1, gy), (inst, gx + 1, gy)
+    odd = lax.rem(gx, 2)
+    mate = (inst, gx + 1 - 2 * odd, gy)
+    outer = odd * (nx - 1)
+    inner = nx - 1 - outer
+    step_out = 2 * odd - 1
+    has_outer = jnp.where(odd == 0, gx > 0, gx < ngx - 1)
+    outside = (lax.rem(inst + 2, ranks), gx + step_out, gy)
     gy_low = (inst, gx, lax.rem(gy + ngy - 1, ngy))
     gy_high = (inst, gx, lax.rem(gy + 1, ngy))
-    has_low, has_high = gx > 0, gx < ngx - 1
-
-    def plane_at(position):
-        half = position // 2
-        odd = position - 2 * half
-        return half + odd * (nx - 1 - 2 * half)
+
+    def outer_at(k):
+        return jnp.minimum(OUTER_FIRST + OUTER_STEP * k, nx - 1)
+
+    def plane_at(position, at):
+        distance = jnp.where(position < at, nx - 1 - position, jnp.where(position > at, nx - position, 0))
+        return outer + (1 - 2 * odd) * distance
 
     def load_state(x):
         return pltpu.make_async_copy(state_ref.at[:, :, x], cur.at[0, x + 1], load_sem.at[x])
@@ -65,28 +73,24 @@
             gy_high if d == 0 else gy_low,
         )
 
-    def gx_copy(k, d):
-        if d == 0:
-            return remote(cur.at[k, nx], cur.at[k, 0], send_sem.at[5], gx_sem.at[k, 0], gx_high)
-        return remote(cur.at[k, 1], cur.at[k, nx + 1], send_sem.at[6], gx_sem.at[k, 1], gx_low)
+    def inner_copy(k):
+        return remote(cur.at[k, inner + 1], cur.at[k, odd * (nx + 1)], send_sem.at[5], gx_sem.at[k, 0], mate)
+
+    def outer_copy(k):
+        return remote(far.at[k, outer], cur.at[k, (1 - odd) * (nx + 1)], send_sem.at[6], gx_sem.at[k, 1], outside)
 
     def send_plane(k, x):
+        @pl.when(x == inner)
+        def _():
+            inner_copy(k).start()
+
         far_copy(k, x).start()
-
-        @pl.when((x == 0) & has_low)
-        def _():
-            gx_copy(k, 1).start()
-
-        @pl.when((x == nx - 1) & has_high)
-        def _():
-            gx_copy(k, 0).start()
-
         near_copy(k, x).start()
         y_copy(k, x, 0).start()
         y_copy(k, x, 1).start()
 
     def start_load(p, c):
-        load_state(plane_at(p)).start()
+        load_state(plane_at(p, 0)).start()
         return c
 
     lax.fori_loop(0, nx, start_load, 0)
@@ -95,22 +99,18 @@
     pltpu.make_async_copy(source_ref, src, src_sem).start()
 
     barrier = pltpu.get_barrier_semaphore()
-    for device in (other_core, other_chip, gy_low, gy_high):
+    for device in (other_core, other_chip, mate, gy_low, gy_high):
         pl.semaphore_signal(barrier, inc=1, device_id=device, device_id_type=MESH)
 
-    @pl.when(has_low)
+    @pl.when(has_outer)
     def _():
-        pl.semaphore_signal(barrier, inc=1, device_id=gx_low, device_id_type=MESH)
-
-    @pl.when(has_high)
-    def _():
-        pl.semaphore_signal(barrier, inc=1, device_id=gx_high, device_id_type=MESH)
+        pl.semaphore_signal(barrier, inc=1, device_id=outside, device_id_type=MESH)
 
     tile = cs.shape[1:]
     for d in range(6):
         for v in range(NV):
             for w in range(NV):
-                cs[(d * NV + v) * NV + w] = jnp.full(tile, coup_ref[d, v, w], jnp.float32)
+                cs[(d * NV + v) * NV + w] = jnp.full(tile, coup_ref[v, d, w], jnp.float32)
     zeros = jnp.zeros(cur.shape[2:], jnp.float32)
 
     @pl.when(gx == 0)
@@ -123,14 +123,14 @@
         for k in range(ITERS):
             cur[k, nx + 1] = zeros
 
-    pl.semaphore_wait(barrier, 4 + has_low.astype(jnp.int32) + has_high.astype(jnp.int32))
+    pl.semaphore_wait(barrier, 5 + has_outer.astype(jnp.int32))
 
     def put_rows(k, x, n, v, plane):
         ysend[k, x, 0, n, v : v + 1, :] = plane[7:8, :]
         ysend[k, x, 1, n, v : v + 1, :] = plane[0:1, :]
 
     def first_send(p, c):
-        x = plane_at(p)
+        x = plane_at(p, 0)
         load_state(x).wait()
         for n in range(nloc):
             for v in range(NV):
@@ -173,30 +173,36 @@
 
     def forward(step):
         k = step // nx
-        x = plane_at(step - k * nx)
-        far_copy(k, x).wait_recv()
-        fwd_copy(k, x).start()
-
-    def output_copies(x):
-        return (
-            pltpu.make_async_copy(cur.at[ITERS, x + 1], out_ref.at[:, :, x], out_sem.at[0, x]),
-            pltpu.make_async_copy(resid.at[x], res_ref.at[:, :, x], out_sem.at[1, x]),
-        )
+        x = plane_at(step - k * nx, outer_at(k))
+
+        @pl.when(x != outer)
+        def _():
+            far_copy(k, x).wait_recv()
+            fwd_copy(k, x).start()
+
+    def forward_outer(k):
+        far_copy(k, outer).wait_recv()
+
+        @pl.when(has_outer)
+        def _():
+            outer_copy(k).start()
+
+        fwd_copy(k, outer).start()
 
     def compute(step):
         k = step // nx
-        x = plane_at(step - k * nx)
+        x = plane_at(step - k * nx, outer_at(k))
         near_copy(k, x).wait_recv()
         y_copy(k, x, 0).wait_recv()
         y_copy(k, x, 1).wait_recv()
 
-        @pl.when((x == 0) & has_low)
-        def _():
-            gx_copy(k, 0).wait_recv()
-
-        @pl.when((x == nx - 1) & has_high)
-        def _():
-            gx_copy(k, 1).wait_recv()
+        @pl.when(x == inner)
+        def _():
+            inner_copy(k).wait_recv()
+
+        @pl.when((x == outer) & has_outer)
+        def _():
+            outer_copy(k).wait_recv()
 
         fwd_copy(k, x).wait_recv()
 
@@ -247,7 +253,7 @@
         for n in range(nloc):
             b = [total_of[n, v] for v in range(NV)]
             for v in range(NV):
-                resid[x, n, v] = b[v]
+                res_ref[n, v, x] = b[v]
             for p in range(NV):
                 for t in range(p + 1, NV):
                     b[t] = b[t] - lu[n, t, p, x] * b[p]
@@ -257,6 +263,7 @@
                 b[p] = b[p] * lu[n, p, p, x]
             for v in range(NV):
                 plane = cur[k, x + 1, n, v] + b[v]
+                out_ref[n, v, x] = plane
                 cur[k + 1, x + 1, n, v] = plane
                 put_rows(k + 1, x, n, v, plane)
 
@@ -264,14 +271,16 @@
         def _():
             send_plane(k + 1, x)
 
-        @pl.when(k == ITERS - 1)
-        def _():
-            for copy in output_copies(x):
-                copy.start()
-
+    forward_outer(0)
     forward(0)
 
     def one_step(step, c):
+        for k in range(1, ITERS):
+
+            @pl.when(step == (k - 1) * nx + outer_at(k - 1) + RELAY_LAG)
+            def _():
+                forward_outer(k)
+
         @pl.when(step + 1 < ITERS * nx)
         def _():
             forward(step + 1)
@@ -289,36 +298,27 @@
         remote(sent, sent, send_sem.at[3 + d], y_sem.at[0, 0, d], gy_high).wait_send()
 
     planes = near.at[0, pl.ds(0, ITERS)]
-
-    @pl.when(has_high)
+    remote(planes, planes, send_sem.at[5], gx_sem.at[0, 0], mate).wait_send()
+
+    @pl.when(has_outer)
     def _():
-        remote(planes, planes, send_sem.at[5], gx_sem.at[0, 0], gx_high).wait_send()
-
-    @pl.when(has_low)
-    def _():
-        remote(planes, planes, send_sem.at[6], gx_sem.at[0, 1], gx_low).wait_send()
-
-    def finish(x, c):
-        for copy in output_copies(x):
-            copy.wait()
-        return c
-
-    lax.fori_loop(0, nx, finish, 0)
+        remote(planes, planes, send_sem.at[6], gx_sem.at[0, 1], outside).wait_send()
 
 
 def shards(state, source, jacobian, couplings, omega):
     nloc, nv, nx, ny, nz = state.shape
-    whole = pl.BlockSpec(memory_space=pl.ANY)
+    whole = pl.BlockSpec(memory_space=pltpu.HBM)
+    in_hbm = functools.partial(pltpu.with_memory_space_constraint, memory_space=pltpu.HBM)
     scalars = pl.BlockSpec(memory_space=pltpu.SMEM)
     f32 = jnp.float32
     dma = pltpu.SemaphoreType.DMA
     plane = (nloc, nv, ny, nz)
-    out = jax.ShapeDtypeStruct(state.shape, f32)
+    out = pltpu.VMEM(state.shape, f32)
     return pl.pallas_call(
         kernel,
         out_shape=(out, out),
         in_specs=[whole, whole, whole, scalars, scalars],
-        out_specs=(whole, whole),
+        out_specs=(pl.BlockSpec(memory_space=pltpu.VMEM),) * 2,
         scratch_shapes=[
             pltpu.VMEM((ITERS + 1, nx + 2) + plane, f32),
             pltpu.VMEM(source.shape, f32),
@@ -329,7 +329,6 @@
             pltpu.VMEM((ITERS, nx) + plane, f32),
             pltpu.VMEM((ITERS + 1, nx, 2, nloc, 8, nz), f32),
             pltpu.VMEM((ITERS, nx, 2, nloc, 8, nz), f32),
-            pltpu.VMEM((nx,) + plane, f32),
             pltpu.VMEM((6 * NV * NV, ny, nz), f32),
             dma((nx,)),
             dma,
@@ -340,10 +339,9 @@
             dma((ITERS, nx, 2)),
             dma((ITERS, 2)),
             dma((7,)),
-            dma((2, nx)),
         ],
-        compiler_params=pltpu.CompilerParams(collective_id=0, has_side_effects=True),
-    )(state, source, jacobian, couplings, omega)
+        compiler_params=pltpu.CompilerParams(collective_id=0, has_side_effects=True, vmem_limit_bytes=24 * 2**20),
+    )(in_hbm(state), in_hbm(source), in_hbm(jacobian), jnp.transpose(couplings, (1, 0, 2)), omega)
 
 
 def solution(mesh):

time: 46.9 us -> 43.1 us (0.919)
  the two profiles are of different devices: /device:TPU:9 before, /device:TPU:1 now
where the time goes in v1:
time: 43.1 us; the launch traced here: 43 us
  Pallas kernels  39.5 us (92%)
  local copies, waits for them, and re-layouts  2.17 us (5%)
  between operations  1.29 us (3%)
    pallas_call x1, Pallas kernels, shards(): pl.pallas_call(kernel, out_shape=(out, out), in_specs=[whole, whole, whol...  39.5 us
    unnamed x4, local copies, waits for them, and re-layouts  2.17 us

profile of v1, /device:TPU:1, one launch (start us, length us, event | category | flops | bytes accessed | tf_op | source)
XLA Modules:
  0.0 43.0 jit_solution(2998629700614823910)
XLA Ops:
  1.3 0.0 copy-start
  1.3 0.7 %copy-done = f32[6,5,5]{2,0,1:T(8,128)S(1)} copy-done((f32[6,5,5]{2,0,1:T(8,128)S(1)}, f32[6,5,5]{2,0,1:T(8,128)}, u32[]{:S(2)}) %copy-start) | copy-done | bytes 624
  2.0 39.5 %shard_map.68 = (f32[2,5,8,8,128]{4,3,2,1,0:T(8,128)S(1)}, f32[2,5,8,8,128]{4,3,2,1,0:T(8,128)S(1)}) custom-call(f32[2,5,8,8,128]{4,3,2,1,0:T(8,128)} %state_ref.1, f32[2,5,8,8,128]{4,3,2,1,0:T(8,128)} %source_ref.1, f32[2,5,5,8,8,128]{5,4,3,2,1,0:T(8,128)} %jac_ref.1, f32[5,6,5]{2,1,0:T(8,128)S(1)} %bitcast.1, f32[1]{0:T(128)S(6)} %copy.11.omega_ref), custom_call_target="tpu_custom_call" | custom-call | tf_op jit(solution)/shard_map/pallas_call | solution.py:317
  41.5 0.7 %copy.9 = f32[2,5,8,8,128]{4,3,2,1,0:T(8,128)} copy(f32[2,5,8,8,128]{4,3,2,1,0:T(8,128)S(1)} %get-tuple-element.2) | data formatting | bytes 655360
  42.2 0.7 %copy.10 = f32[2,5,8,8,128]{4,3,2,1,0:T(8,128)} copy(f32[2,5,8,8,128]{4,3,2,1,0:T(8,128)S(1)} %get-tuple-element.3) | data formatting | bytes 655360
Async XLA Ops:
  1.3 0.7 %copy-start = (f32[6,5,5]{2,0,1:T(8,128)S(1)}, f32[6,5,5]{2,0,1:T(8,128)}, u32[]{:S(2)}) copy-start(f32[6,5,5]{2,0,1:T(8,128)} %param.8) | copy-start | bytes 1804

commit v2 on v1

--- a/solution.py
+++ b/solution.py
@@ -22,8 +22,8 @@
 def kernel(
     state_ref, source_ref, jac_ref, coup_ref, omega_ref,
     out_ref, res_ref,
-    cur, src, jac, lu, near, far, fwd, ysend, yrecv, cs,
-    load_sem, src_sem, jac_sem, near_sem, far_sem, fwd_sem, y_sem, gx_sem, send_sem,
+    cur, src, jac, lu, near, far, fwd, ysend, yrecv, cs, coup,
+    load_sem, src_sem, jac_sem, near_sem, far_sem, fwd_sem, y_sem, gx_sem, send_sem, coup_sem, group_sem,
 ):
     inst, gx, gy = lax.axis_index("inst"), lax.axis_index("gx"), lax.axis_index("gy")
     ngx, ngy, ranks = lax.axis_size("gx"), lax.axis_size("gy"), lax.axis_size("inst")
@@ -86,9 +86,12 @@
 
         far_copy(k, x).start()
         near_copy(k, x).start()
+
+    def send_rows(k, x):
         y_copy(k, x, 0).start()
         y_copy(k, x, 1).start()
 
+    pltpu.make_async_copy(coup_ref, coup, coup_sem).start()
     def start_load(p, c):
         load_state(plane_at(p, 0)).start()
         return c
@@ -98,19 +101,75 @@
         pltpu.make_async_copy(jac_ref.at[n], jac.at[n], jac_sem.at[n]).start()
     pltpu.make_async_copy(source_ref, src, src_sem).start()
 
+    even_here, odd_here = (inst - parity, gx, gy), (inst - parity + 1, gx, gy)
+    even_far = (lax.rem(inst - parity + 2, ranks), gx, gy)
+
+    def odd_core(device):
+        return (device[0] - parity + 1, device[1], device[2])
+
     barrier = pltpu.get_barrier_semaphore()
-    for device in (other_core, other_chip, mate, gy_low, gy_high):
+
+    def greet(device):
         pl.semaphore_signal(barrier, inc=1, device_id=device, device_id_type=MESH)
 
+    greet(even_far)
+
+    @pl.when(parity == 1)
+    def _():
+        greet(even_here)
+
+    for device in (mate, gy_low, gy_high):
+        greet(odd_core(device))
+
     @pl.when(has_outer)
     def _():
-        pl.semaphore_signal(barrier, inc=1, device_id=outside, device_id_type=MESH)
+        greet(odd_core(outside))
+
+    @pl.when(parity == 0)
+    def _():
+        pl.semaphore_wait(barrier, 3)
+        pl.semaphore_signal(group_sem, inc=1, device_id=odd_here, device_id_type=MESH)
+
+    @pl.when(parity == 1)
+    def _():
+        pl.semaphore_wait(group_sem, 1)
+
+    def meet_neighbours():
+        @pl.when(parity == 1)
+        def _():
+            pl.semaphore_wait(barrier, 6 + 2 * has_outer.astype(jnp.int32))
+            pl.semaphore_signal(group_sem, inc=1, device_id=even_here, device_id_type=MESH)
+
+        @pl.when(parity == 0)
+        def _():
+            pl.semaphore_wait(group_sem, 1)
+
+    def put_rows(k, x, n, v, plane):
+        ysend[k, x, 0, n, v : v + 1, :] = plane[7:8, :]
+        ysend[k, x, 1, n, v : v + 1, :] = plane[0:1, :]
+
+    def first_send(p, c):
+        x = plane_at(p, 0)
+        load_state(x).wait()
+        far_copy(0, x).start()
+        near_copy(0, x).start()
+        for n in range(nloc):
+            for v in range(NV):
+                put_rows(0, x, n, v, cur[0, x + 1, n, v])
+        return c
+
+    def first_rows(p, c):
+        send_rows(0, plane_at(p, 0))
+        return c
+
+    lax.fori_loop(0, nx, first_send, 0)
 
     tile = cs.shape[1:]
+    pltpu.make_async_copy(coup_ref, coup, coup_sem).wait()
     for d in range(6):
         for v in range(NV):
             for w in range(NV):
-                cs[(d * NV + v) * NV + w] = jnp.full(tile, coup_ref[v, d, w], jnp.float32)
+                cs[(d * NV + v) * NV + w] = jnp.full(tile, coup[v, d, w], jnp.float32)
     zeros = jnp.zeros(cur.shape[2:], jnp.float32)
 
     @pl.when(gx == 0)
@@ -122,23 +181,6 @@
     def _():
         for k in range(ITERS):
             cur[k, nx + 1] = zeros
-
-    pl.semaphore_wait(barrier, 5 + has_outer.astype(jnp.int32))
-
-    def put_rows(k, x, n, v, plane):
-        ysend[k, x, 0, n, v : v + 1, :] = plane[7:8, :]
-        ysend[k, x, 1, n, v : v + 1, :] = plane[0:1, :]
-
-    def first_send(p, c):
-        x = plane_at(p, 0)
-        load_state(x).wait()
-        for n in range(nloc):
-            for v in range(NV):
-                put_rows(0, x, n, v, cur[0, x + 1, n, v])
-        send_plane(0, x)
-        return c
-
-    lax.fori_loop(0, nx, first_send, 0)
 
     for n in range(nloc):
         pltpu.make_async_copy(jac_ref.at[n], jac.at[n], jac_sem.at[n]).wait()
@@ -159,6 +201,9 @@
 
     lax.fori_loop(0, nx, factor, 0)
     pltpu.make_async_copy(source_ref, src, src_sem).wait()
+    meet_neighbours()
+    inner_copy(0).start()
+    lax.fori_loop(0, nx, first_rows, 0)
 
     omega = omega_ref[0]
 
@@ -270,6 +315,7 @@
         @pl.when(k < ITERS - 1)
         def _():
             send_plane(k + 1, x)
+            send_rows(k + 1, x)
 
     forward_outer(0)
     forward(0)
@@ -314,10 +360,10 @@
     dma = pltpu.SemaphoreType.DMA
     plane = (nloc, nv, ny, nz)
     out = pltpu.VMEM(state.shape, f32)
-    return pl.pallas_call(
+    results = pl.pallas_call(
         kernel,
         out_shape=(out, out),
-        in_specs=[whole, whole, whole, scalars, scalars],
+        in_specs=[whole, whole, whole, whole, scalars],
         out_specs=(pl.BlockSpec(memory_space=pltpu.VMEM),) * 2,
         scratch_shapes=[
             pltpu.VMEM((ITERS + 1, nx + 2) + plane, f32),
@@ -330,6 +376,7 @@
             pltpu.VMEM((ITERS + 1, nx, 2, nloc, 8, nz), f32),
             pltpu.VMEM((ITERS, nx, 2, nloc, 8, nz), f32),
             pltpu.VMEM((6 * NV * NV, ny, nz), f32),
+            pltpu.SMEM((NV, 6, NV), f32),
             dma((nx,)),
             dma,
             dma((nloc,)),
@@ -339,9 +386,30 @@
             dma((ITERS, nx, 2)),
             dma((ITERS, 2)),
             dma((7,)),
+            dma,
+            pltpu.SemaphoreType.REGULAR,
         ],
         compiler_params=pltpu.CompilerParams(collective_id=0, has_side_effects=True, vmem_limit_bytes=24 * 2**20),
-    )(in_hbm(state), in_hbm(source), in_hbm(jacobian), jnp.transpose(couplings, (1, 0, 2)), omega)
+    )(in_hbm(state), in_hbm(source), in_hbm(jacobian), in_hbm(jnp.transpose(couplings, (1, 0, 2))), omega)
+    in_vmem = pl.BlockSpec(memory_space=pltpu.VMEM)
+    return pl.pallas_call(
+        write_out,
+        out_shape=(jax.ShapeDtypeStruct(state.shape, f32),) * 2,
+        in_specs=[in_vmem, in_vmem],
+        out_specs=(pl.BlockSpec(memory_space=pl.ANY),) * 2,
+        scratch_shapes=[dma((2,))],
+    )(*(pltpu.with_memory_space_constraint(r, pltpu.VMEM) for r in results))
+
+
+def write_out(next_ref, resid_ref, out_ref, res_ref, sems):
+    copies = [
+        pltpu.make_async_copy(next_ref, out_ref, sems.at[0]),
+        pltpu.make_async_copy(resid_ref, res_ref, sems.at[1]),
+    ]
+    for copy in copies:
+        copy.start()
+    for copy in copies:
+        copy.wait()
 
 
 def solution(mesh):

time: 43.1 us -> 39.8 us (0.923)
  local copies, waits for them, and re-layouts: 2.17 us -> 0 us
  Pallas kernels: 39.5 us -> 38.4 us
    unnamed x4 -> x0, local copies, waits for them, and re-layouts: 2.17 us -> none
    pallas_call x1, Pallas kernels: 39.5 us -> 37.6 us  [shards(): pl.pallas_call(kernel, out_shape=(out, out), in_specs=[whole, whole, whol...]
    pallas_call x0 -> x1, Pallas kernels: none -> 0.85 us  [shards(): pl.pallas_call(write_out, out_shape=(jax.ShapeDtypeStruct(state.shape, f3...]
where the time goes in v2:
time: 39.8 us; the launch traced here: 39.7 us
  Pallas kernels  38.4 us (96%)
  between operations  1.29 us (3%)
    pallas_call x1, Pallas kernels, shards(): pl.pallas_call(kernel, out_shape=(out, out), in_specs=[whole, whole, whol...  37.6 us
    pallas_call x1, Pallas kernels, shards(): pl.pallas_call(write_out, out_shape=(jax.ShapeDtypeStruct(state.shape, f3...  0.85 us

profile of v2, /device:TPU:1, one launch (start us, length us, event | category | flops | bytes accessed | tf_op | source)
XLA Modules:
  0.0 39.7 jit_solution(6420644204370254531)
XLA Ops:
  1.3 37.6 %shard_map.68 = (f32[2,5,8,8,128]{4,3,2,1,0:T(8,128)S(1)}, f32[2,5,8,8,128]{4,3,2,1,0:T(8,128)S(1)}) custom-call(f32[2,5,8,8,128]{4,3,2,1,0:T(8,128)} %state_ref.1, f32[2,5,8,8,128]{4,3,2,1,0:T(8,128)} %source_ref.1, f32[2,5,5,8,8,128]{5,4,3,2,1,0:T(8,128)} %jac_ref.1, f32[5,6,5]{2,1,0:T(8,128)} %bitcast.1, f32[1]{0:T(128)S(6)} %copy.7.omega_ref), custom_call_target="tpu_custom_call" | custom-call | tf_op jit(solution)/shard_map/pallas_call | solution.py:363
  38.9 0.9 %shard_map.69 = (f32[2,5,8,8,128]{4,3,2,1,0:T(8,128)}, f32[2,5,8,8,128]{4,3,2,1,0:T(8,128)}) custom-call(f32[2,5,8,8,128]{4,3,2,1,0:T(8,128)S(1)} %get-tuple-element.4.next_ref, f32[2,5,8,8,128]{4,3,2,1,0:T(8,128)S(1)} %get-tuple-element.5.resid_ref), custom_call_target="tpu_custom_call" | custom-call | tf_op jit(solution)/shard_map/pallas_call | solution.py:395

commit v3 on v2

--- a/solution.py
+++ b/solution.py
@@ -9,7 +9,8 @@
 from jax.sharding import PartitionSpec as P
 
 ITERS = 3
-OUTER_FIRST, OUTER_STEP, RELAY_LAG = 3, 2, 4
+EARLY = 4
+OUTER_FIRST, OUTER_STEP, RELAY_LAG = 3, 2, 5
 NV = 5
 MESH = pl.DeviceIdType.MESH
 
@@ -153,16 +154,17 @@
         load_state(x).wait()
         far_copy(0, x).start()
         near_copy(0, x).start()
+        return c
+
+    def first_rows(p, c):
+        x = plane_at(p, 0)
         for n in range(nloc):
             for v in range(NV):
                 put_rows(0, x, n, v, cur[0, x + 1, n, v])
+        send_rows(0, x)
         return c
 
-    def first_rows(p, c):
-        send_rows(0, plane_at(p, 0))
-        return c
-
-    lax.fori_loop(0, nx, first_send, 0)
+    lax.fori_loop(0, EARLY, first_send, 0)
 
     tile = cs.shape[1:]
     pltpu.make_async_copy(coup_ref, coup, coup_sem).wait()
@@ -203,6 +205,7 @@
     pltpu.make_async_copy(source_ref, src, src_sem).wait()
     meet_neighbours()
     inner_copy(0).start()
+    lax.fori_loop(EARLY, nx, first_send, 0)
     lax.fori_loop(0, nx, first_rows, 0)
 
     omega = omega_ref[0]
@@ -248,8 +251,6 @@
         @pl.when((x == outer) & has_outer)
         def _():
             outer_copy(k).wait_recv()
-
-        fwd_copy(k, x).wait_recv()
 
         lane = lax.broadcasted_iota(jnp.int32, tile, 1)
         row = lax.broadcasted_iota(jnp.int32, tile, 0)
@@ -283,6 +284,7 @@
                     c = cs[(d * NV + v) * NV + w]
                     for n in range(nloc):
                         total_of[n, v] = total_of[n, v] - c * field[n, w]
+        fwd_copy(k, x).wait_recv()
         for v in range(NV):
             own = [cur[k, x + 1, m, v] for m in range(nloc)]
             beside = [near[k, x, m, v] for m in range(nloc)]

time: 39.8 us -> 36.7 us (0.922)
  Pallas kernels: 38.4 us -> 35.3 us
    pallas_call x1, Pallas kernels: 37.6 us -> 34.4 us  [shards(): pl.pallas_call(kernel, out_shape=(out, out), in_specs=[whole, whole, whol...]
where the time goes in v3:
time: 36.7 us; the launch traced here: 36.6 us
  Pallas kernels  35.3 us (96%)
  between operations  1.29 us (4%)
    pallas_call x1, Pallas kernels, shards(): pl.pallas_call(kernel, out_shape=(out, out), in_specs=[whole, whole, whol...  34.4 us
    pallas_call x1, Pallas kernels, shards(): pl.pallas_call(write_out, out_shape=(jax.ShapeDtypeStruct(state.shape, f3...  0.85 us

profile of v3, /device:TPU:1, one launch (start us, length us, event | category | flops | bytes accessed | tf_op | source)
XLA Modules:
  0.0 36.6 jit_solution(16523486614513151397)
XLA Ops:
  1.3 34.4 %shard_map.68 = (f32[2,5,8,8,128]{4,3,2,1,0:T(8,128)S(1)}, f32[2,5,8,8,128]{4,3,2,1,0:T(8,128)S(1)}) custom-call(f32[2,5,8,8,128]{4,3,2,1,0:T(8,128)} %state_ref.1, f32[2,5,8,8,128]{4,3,2,1,0:T(8,128)} %source_ref.1, f32[2,5,5,8,8,128]{5,4,3,2,1,0:T(8,128)} %jac_ref.1, f32[5,6,5]{2,1,0:T(8,128)} %bitcast.1, f32[1]{0:T(128)S(6)} %copy.7.omega_ref), custom_call_target="tpu_custom_call" | custom-call | tf_op jit(solution)/shard_map/pallas_call | solution.py:365
  35.7 0.9 %shard_map.69 = (f32[2,5,8,8,128]{4,3,2,1,0:T(8,128)}, f32[2,5,8,8,128]{4,3,2,1,0:T(8,128)}) custom-call(f32[2,5,8,8,128]{4,3,2,1,0:T(8,128)S(1)} %get-tuple-element.4.next_ref, f32[2,5,8,8,128]{4,3,2,1,0:T(8,128)S(1)} %get-tuple-element.5.resid_ref), custom_call_target="tpu_custom_call" | custom-call | tf_op jit(solution)/shard_map/pallas_call | solution.py:397

commit v4 on v3

--- a/solution.py
+++ b/solution.py
@@ -284,19 +284,23 @@
                     c = cs[(d * NV + v) * NV + w]
                     for n in range(nloc):
                         total_of[n, v] = total_of[n, v] - c * field[n, w]
-        fwd_copy(k, x).wait_recv()
         for v in range(NV):
             own = [cur[k, x + 1, m, v] for m in range(nloc)]
             beside = [near[k, x, m, v] for m in range(nloc)]
             across = [far[k, x, m, v] for m in range(nloc)]
-            relayed = [fwd[k, x, m, v] for m in range(nloc)]
             for j in range(nloc):
                 acc = total_of[j, v]
-                for weights, values in ((own_w, own), (near_w, beside), (far_w, across), (fwd_w, relayed)):
+                for weights, values in ((own_w, own), (near_w, beside), (far_w, across)):
                     for m in range(nloc):
                         if weights[j][m] is not None:
                             acc = acc - weights[j][m] * values[m]
                 total_of[j, v] = acc
+        fwd_copy(k, x).wait_recv()
+        for v in range(NV):
+            relayed = [fwd[k, x, m, v] for m in range(nloc)]
+            for j in range(nloc):
+                for m in range(nloc):
+                    total_of[j, v] = total_of[j, v] - fwd_w[j][m] * relayed[m]
         for n in range(nloc):
             b = [total_of[n, v] for v in range(NV)]
             for v in range(NV):
@@ -312,10 +316,11 @@
                 plane = cur[k, x + 1, n, v] + b[v]
                 out_ref[n, v, x] = plane
                 cur[k + 1, x + 1, n, v] = plane
-                put_rows(k + 1, x, n, v, plane)
 
         @pl.when(k < ITERS - 1)
         def _():
+            for n, v in pairs:
+                put_rows(k + 1, x, n, v, cur[k + 1, x + 1, n, v])
             send_plane(k + 1, x)
             send_rows(k + 1, x)
 

time: 36.7 us -> 36.7 us (level)
  no operation moved by 1% of the time
where the time goes in v4:
time: 36.7 us; the launch traced here: 36.5 us
  Pallas kernels  35.2 us (96%)
  between operations  1.29 us (4%)
    pallas_call x1, Pallas kernels, shards(): pl.pallas_call(kernel, out_shape=(out, out), in_specs=[whole, whole, whol...  34.4 us
    pallas_call x1, Pallas kernels, shards(): pl.pallas_call(write_out, out_shape=(jax.ShapeDtypeStruct(state.shape, f3...  0.85 us

profile of v4, /device:TPU:1, one launch (start us, length us, event | category | flops | bytes accessed | tf_op | source)
XLA Modules:
  0.0 36.5 jit_solution(10642816449987785162)
XLA Ops:
  1.3 34.4 %shard_map.68 = (f32[2,5,8,8,128]{4,3,2,1,0:T(8,128)S(1)}, f32[2,5,8,8,128]{4,3,2,1,0:T(8,128)S(1)}) custom-call(f32[2,5,8,8,128]{4,3,2,1,0:T(8,128)} %state_ref.1, f32[2,5,8,8,128]{4,3,2,1,0:T(8,128)} %source_ref.1, f32[2,5,5,8,8,128]{5,4,3,2,1,0:T(8,128)} %jac_ref.1, f32[5,6,5]{2,1,0:T(8,128)} %bitcast.1, f32[1]{0:T(128)S(6)} %copy.7.omega_ref), custom_call_target="tpu_custom_call" | custom-call | tf_op jit(solution)/shard_map/pallas_call | solution.py:370
  35.7 0.9 %shard_map.69 = (f32[2,5,8,8,128]{4,3,2,1,0:T(8,128)}, f32[2,5,8,8,128]{4,3,2,1,0:T(8,128)}) custom-call(f32[2,5,8,8,128]{4,3,2,1,0:T(8,128)S(1)} %get-tuple-element.4.next_ref, f32[2,5,8,8,128]{4,3,2,1,0:T(8,128)S(1)} %get-tuple-element.5.resid_ref), custom_call_target="tpu_custom_call" | custom-call | tf_op jit(solution)/shard_map/pallas_call | solution.py:402
